TPU v7x, 32 devices: a whole 2x2x4 slice. The times are simulated.
32 devices in a mesh: group: 2 (over y), section: 4 (over x, core), tensor: 4 (over z).
Axes of the slice: x: 2, y: 2, z: 4, core: 2. Of those that a mesh axis runs over, the one named last changes fastest.
Arguments:
- hidden_states: bfloat16 [2, 4, 4, 8192], P('group', 'section', 'tensor'), may hold values from -6 to 6
- query_train: bfloat16 [4, 8192, 4096], P(None, ('group', 'section'), 'tensor'), may hold values from -0.0625 to 0.0625
- keyval_train: bfloat16 [4, 8192, 1024], P(None, ('group', 'section'), 'tensor'), may hold values from -0.0625 to 0.0625
- layer_of_section: int32 [4], replicated, may hold values from 0 to 3, each once
- lengths: int32 [2, 4, 4], P('group', 'section', 'tensor'), may hold values from 2 to 1024
- kv_cache: bfloat16 [2, 4, 4, 1024, 1024], P('group', 'section', 'tensor'), as said below
Outputs:
- attended: bfloat16 [2, 4, 4, 4096], P('group', 'section', 'tensor')
- new_entries: bfloat16 [2, 4, 4, 1024], P('group', 'section', 'tensor')
Inputs may be any that keep to these rules, and one draw needn't show every extreme that they name: `layer_of_section`: every layer appears once. `kv_cache`: cache positions at or past a sequence's length hold entries that are never read.
All inputs are finite; a program needn't handle non-finite values.
Results may differ from a plain program's by a relative error of at most 0.03.
Values may be sent and summed in bfloat16 or wider, within the bound.
A program may use at most 64 MiB of HBM per device.

v0:
```python
import jax
import jax.numpy as jnp
from jax import lax
from jax.sharding import PartitionSpec as P

HD = 128
QH = 32
KVH = 4


def rotate(vectors, position):
    half_size = HD // 2
    inverse = jnp.power(jnp.float32(500000.0), -jnp.arange(half_size, dtype=jnp.float32) * 2.0 / HD)
    angle = position[:, None, None] * inverse[None, None, :]
    cosine = jnp.cos(angle)
    sine_part = jnp.sin(angle)
    first_half = vectors[..., :half_size]
    second = vectors[..., half_size:]
    return jnp.concatenate(
        [first_half * cosine - second * sine_part, second * cosine + first_half * sine_part],
        axis=-1,
    )


def attend(queries, key_value, seq_lens, cache):
    count = queries.shape[0]
    cache_len = cache.shape[1]
    per_kv = QH // KVH
    position = seq_lens.astype(jnp.float32)
    query_rot = rotate(queries.astype(jnp.float32).reshape(count, QH, HD), position).astype(
        jnp.bfloat16
    )
    key_rot = rotate(
        key_value[:, : KVH * HD].astype(jnp.float32).reshape(count, KVH, HD), position
    ).astype(jnp.bfloat16)
    new_values = key_value[:, KVH * HD :]
    cache_keys = cache[:, :, : KVH * HD].reshape(count, cache_len, KVH, HD)
    cache_values = cache[:, :, KVH * HD :].reshape(count, cache_len, KVH, HD)
    query_group = query_rot.reshape(count, KVH, per_kv, HD)
    score_scale = 1.0 / jnp.sqrt(jnp.float32(HD))
    scores = (
        jnp.einsum("skgd,sjkd->skgj", query_group, cache_keys, preferred_element_type=jnp.float32)
        * score_scale
    )
    own_score = (
        jnp.einsum("skgd,skd->skg", query_group, key_rot, preferred_element_type=jnp.float32)
        * score_scale
    )
    usable = (jnp.arange(cache_len, dtype=jnp.int32)[None, :] < seq_lens[:, None])[:, None, None, :]
    scores = jnp.where(usable, scores, jnp.float32(-1e30))
    largest = jnp.maximum(jnp.max(scores, axis=-1), own_score)
    exponent = jnp.where(usable, jnp.exp(scores - largest[..., None]), jnp.float32(0.0))
    own_exp = jnp.exp(own_score - largest)
    totals = jnp.sum(exponent, axis=-1) + own_exp
    probs = (exponent / totals[..., None]).astype(jnp.bfloat16)
    own_prob = (own_exp / totals).astype(jnp.bfloat16)
    new_float = new_values.astype(jnp.float32).reshape(count, KVH, HD)
    result = jnp.einsum("skgj,sjkd->skgd", probs, cache_values, preferred_element_type=jnp.float32)
    result = result + own_prob.astype(jnp.float32)[..., None] * new_float[:, :, None, :]
    entries = jnp.concatenate([key_rot.reshape(count, KVH * HD), new_values], axis=1)
    return (result.reshape(count, QH * HD).astype(jnp.bfloat16), entries)


def shards(hidden_states, query_train, keyval_train, layer_of_section, lengths, kv_cache):
    all_tokens = lax.all_gather(hidden_states[0, 0], "tensor", axis=0, tiled=True)
    query_sorted = query_train[layer_of_section]
    keyval_sorted = keyval_train[layer_of_section]
    moved = (
        lax.all_to_all(query_sorted, "section", split_axis=0, concat_axis=1, tiled=True),
        lax.all_to_all(keyval_sorted, "section", split_axis=0, concat_axis=1, tiled=True),
    )
    query_cols = moved[0].shape[2]
    batch_rows = all_tokens.shape[0]
    group_count = lax.axis_size("group")
    row_count = moved[0].shape[1]
    blocks = all_tokens.reshape(1, batch_rows, group_count, row_count)
    arrived = lax.all_to_all(blocks, "group", split_axis=2, concat_axis=0, tiled=True)
    w_both = jnp.concatenate([moved[0][0], moved[1][0]], axis=1)
    both_parts = lax.psum_scatter(
        jnp.einsum("gbr,rc->gbc", arrived[:, :, 0, :], w_both, preferred_element_type=jnp.float32),
        "group",
        scatter_dimension=0,
        tiled=True,
    )[0]
    query_part = both_parts[:, :query_cols]
    keyval_part = both_parts[:, query_cols:]
    queries = query_part.astype(jnp.bfloat16)
    key_value = keyval_part.astype(jnp.bfloat16)
    query_seq, keyval_seq = (
        lax.all_to_all(queries, "tensor", split_axis=0, concat_axis=1, tiled=True),
        lax.all_to_all(key_value, "tensor", split_axis=0, concat_axis=1, tiled=True),
    )
    result, entries = attend(query_seq, keyval_seq, lengths[0, 0], kv_cache[0, 0])
    return (result[None, None], entries[None, None])


def solution(mesh):
    in_specs = (
        P("group", "section", "tensor", None),
        P(None, ("group", "section"), "tensor"),
        P(None, ("group", "section"), "tensor"),
        P(),
        P("group", "section", "tensor"),
        P("group", "section", "tensor", None, None),
    )
    out_specs = (P("group", "section", "tensor", None), P("group", "section", "tensor", None))
    return jax.shard_map(shards, mesh=mesh, in_specs=in_specs, out_specs=out_specs, check_vma=False)
```

profile of v0, /device:TPU:0, one launch (start us, length us, event | category | flops | bytes accessed | tf_op | source)
XLA Modules:
  0.0 190.8 jit_solution(7543319990391198501)
XLA Ops:
  0.6 0.0 copy-start
  0.6 15.4 %all-gather = bf16[4,1,1,8192]{3,2,1,0:T(2,128)(2,1)S(1)} all-gather(bf16[1,1,1,8192]{3,2,1,0:T(2,128)(2,1)} %param.6), channel_id=2, replica_groups=mesh['group'=2,'section'=4,'tensor'=4] {'tensor'}, dimensions={0}, use_global_device_ids=true | all-gather | bytes 81920 | tf_op jit(solution)/shard_map/all_gather | solution.py:65
  16.1 1.0 reduce.4
  17.1 3.3 %all-to-all-start.2 = ((bf16[1,4,2,4096]{3,1,0,2:T(4,128)(2,1)}), bf16[1,4,2,4096]{3,1,0,2:T(4,128)(2,1)S(1)}, u32[]{:S(2)}, u32[]{:S(2)}) async-start(bf16[1,4,2,4096]{3,1,0,2:T(4,128)(2,1)} %bitcast.30), calls=%async_computation.2 | async-start | bytes 131072 | tf_op jit(solution)/shard_map/all_to_all | solution.py:77
  20.4 0.7 compare_select_fusion
  21.0 0.0 copy-done
  21.1 2.0 %gather_fusion = bf16[4,1024,256]{2,1,0:T(8,128)(2,1)} fusion(bf16[4,1024,256]{2,1,0:T(8,128)(2,1)S(1)} %copy-done, s32[1024]{0:T(1024)S(1)} %pad_clamp_fusion), kind=kCustom, calls=%fused_computation | custom fusion | bytes 4194320 | tf_op jit(solution)/shard_map/gather | solution.py:67
  23.0 1.4 all-to-all-done.2
  24.5 4.4 %all-to-all-start.1 = ((bf16[4,1024,256]{2,1,0:T(8,128)(2,1)}), bf16[4,1024,256]{2,1,0:T(8,128)(2,1)}, u32[]{:S(2)}, u32[]{:S(2)}) async-start(bf16[4,1024,256]{2,1,0:T(8,128)(2,1)} %gather_fusion), calls=%async_computation.1 | async-start | bytes 4194304 | tf_op jit(solution)/shard_map/all_to_all | solution.py:70
  28.9 5.9 %fusion.23 = (bf16[4,512,1024]{2,1,0:T(8,128)(2,1)}, bf16[4,512,1024]{2,1,0:T(8,128)(2,1)}) fusion(bf16[4,1024,1024]{2,1,0:T(8,128)(2,1)} %param.7), kind=kLoop, calls=%fused_computation.53 | loop fusion | bytes 16777216 | tf_op jit(solution)/shard_map/gather | solution.py:66
  34.8 5.0 %gather_fusion.1 = bf16[4,512,1024]{2,1,0:T(8,128)(2,1)} fusion(bf16[4,512,1024]{2,1,0:T(8,128)(2,1)} %get-tuple-element.2, s32[1024]{0:T(1024)S(1)} %pad_clamp_fusion), kind=kCustom, calls=%fused_computation.1 | custom fusion | bytes 8388624 | tf_op jit(solution)/shard_map/gather | solution.py:66
  39.8 4.9 %gather_fusion.2 = bf16[4,512,1024]{2,1,0:T(8,128)(2,1)} fusion(bf16[4,512,1024]{2,1,0:T(8,128)(2,1)} %get-tuple-element.3, s32[1024]{0:T(1024)S(1)} %pad_clamp_fusion), kind=kCustom, calls=%fused_computation.2 | custom fusion | bytes 8388624 | tf_op jit(solution)/shard_map/gather | solution.py:66
  44.7 7.7 %pad_maximum_fusion = bf16[4,1024,1024]{2,1,0:T(8,128)(2,1)} fusion(bf16[4,512,1024]{2,1,0:T(8,128)(2,1)} %gather_fusion.2, bf16[4,512,1024]{2,1,0:T(8,128)(2,1)} %gather_fusion.1), kind=kLoop, calls=%fused_computation.5 | loop fusion | flops 16777216 | bytes 16777216
  52.4 2.3 %all-to-all-done.1 = bf16[4,1024,256]{2,1,0:T(8,128)(2,1)} async-done(((bf16[4,1024,256]{2,1,0:T(8,128)(2,1)}), bf16[4,1024,256]{2,1,0:T(8,128)(2,1)}, u32[]{:S(2)}, u32[]{:S(2)}) %all-to-all-start.1) | async-done | bytes 2097184 | tf_op jit(solution)/shard_map/all_to_all | solution.py:70
  54.7 5.7 %all-to-all-start = ((bf16[4,1024,1024]{2,1,0:T(8,128)(2,1)}), bf16[4,1024,1024]{2,1,0:T(8,128)(2,1)}, u32[]{:S(2)}, u32[]{:S(2)}) async-start(bf16[4,1024,1024]{2,1,0:T(8,128)(2,1)} %pad_maximum_fusion), calls=%async_computation | async-start | bytes 16777216 | tf_op jit(solution)/shard_map/all_to_all | solution.py:69
  60.4 0.0 copy-start.1
  61.0 3.9 %copy.14 = bf16[1,1,1,1024,1024]{3,4,2,1,0:T(8,128)(2,1)} copy(bf16[1,1,1,1024,1024]{4,3,2,1,0:T(8,128)(2,1)} %param.11) | data formatting | bytes 4194304 | tf_op args[5]
  65.0 0.0 copy-done.1
  65.0 0.6 dynamic-slice
  65.6 2.7 %fusion.24 = (bf16[1,1024,512]{1,2,0:T(8,128)(2,1)}, bf16[1,1024,512]{1,2,0:T(8,128)(2,1)S(1)}) fusion(bf16[1,1024,1024]{1,2,0:T(8,128)(2,1)} %bitcast.53), kind=kLoop, calls=%fused_computation.54 | loop fusion | bytes 4194304 | tf_op jit(solution)/shard_map/slice | solution.py:37
  68.3 85.2 %all-to-all-done = bf16[4,1024,1024]{2,1,0:T(8,128)(2,1)} async-done(((bf16[4,1024,1024]{2,1,0:T(8,128)(2,1)}), bf16[4,1024,1024]{2,1,0:T(8,128)(2,1)}, u32[]{:S(2)}, u32[]{:S(2)}) %all-to-all-start) | async-done | bytes 8388640 | tf_op jit(solution)/shard_map/all_to_all | solution.py:69
  153.5 4.9 %fusion.1 = f32[2,4,1280]{2,1,0:T(4,128)S(1)} fusion(bf16[4096,256]{1,0:T(8,128)(2,1)} %bitcast.2, bf16[4096,1024]{1,0:T(8,128)(2,1)} %bitcast.1, bf16[1,4,2,4096]{3,1,0,2:T(4,128)(2,1)S(1)} %all-to-all-done.2), kind=kOutput, calls=%fused_computation.6 | convolution fusion | flops 104857600 | bytes 10592256 | tf_op jit(solution)/shard_map/gbr,rc->gbc/dot_general | solution.py:80
  158.4 7.6 %all-reduce = bf16[2,4,1280]{2,1,0:T(4,128)(2,1)S(1)} all-reduce(f32[2,4,1280]{2,1,0:T(4,128)S(1)} %fusion.1), channel_id=3, replica_groups=mesh['group'=2,'section'=4,'tensor'=4] {'group'}, use_global_device_ids=true, to_apply=%region_0.0.clone | all-reduce | flops 10240 | bytes 61440
  165.9 0.7 fusion.10
  166.6 0.5 broadcast.87
  167.1 0.7 reduce.6
  167.8 0.6 reshape.255
  168.4 5.0 %all-to-all-start.4 = ((bf16[4,2,128]{2,1,0:T(2,128)(2,1)}), bf16[4,2,128]{2,1,0:T(2,128)(2,1)S(1)}, u32[]{:S(2)}, u32[]{:S(2)}) async-start(bf16[4,2,128]{2,1,0:T(2,128)(2,1)} %reshape.255), calls=%async_computation.4 | async-start | bytes 4096 | tf_op jit(solution)/shard_map/all_to_all | solution.py:91
  173.3 0.7 reduce.5
  174.0 0.6 reshape.253
  174.6 4.2 %all-to-all-done.4 = bf16[4,2,128]{2,1,0:T(2,128)(2,1)S(1)} async-done(((bf16[4,2,128]{2,1,0:T(2,128)(2,1)}), bf16[4,2,128]{2,1,0:T(2,128)(2,1)S(1)}, u32[]{:S(2)}, u32[]{:S(2)}) %all-to-all-start.4) | async-done | bytes 2080 | tf_op jit(solution)/shard_map/all_to_all | solution.py:91
  178.8 3.2 %all-to-all-start.3 = ((bf16[4,2,512]{2,1,0:T(2,128)(2,1)}), bf16[4,2,512]{2,1,0:T(2,128)(2,1)S(1)}, u32[]{:S(2)}, u32[]{:S(2)}) async-start(bf16[4,2,512]{2,1,0:T(2,128)(2,1)} %reshape.253), calls=%async_computation.3 | async-start | bytes 16384 | tf_op jit(solution)/shard_map/all_to_all | solution.py:90
  182.1 0.1 subtract_convert_fusion.1
  182.2 0.1 maximum_bitcast_fusion.6
  182.3 0.6 maximum_bitcast_fusion.4
  182.9 0.1 maximum_bitcast_fusion.5
  183.0 4.7 %all-to-all-done.3 = bf16[4,2,512]{2,1,0:T(2,128)(2,1)S(1)} async-done(((bf16[4,2,512]{2,1,0:T(2,128)(2,1)}), bf16[4,2,512]{2,1,0:T(2,128)(2,1)S(1)}, u32[]{:S(2)}, u32[]{:S(2)}) %all-to-all-start.3) | async-done | bytes 8224 | tf_op jit(solution)/shard_map/all_to_all | solution.py:90
  187.7 0.1 fusion.11
  187.8 0.2 fusion.13
  188.0 1.6 fusion.26
  189.6 0.2 fusion.4
  189.8 0.4 fusion.3
  190.2 0.6 convert_element_type.77
  (12 shorter events, 0.2 us)
Async XLA Ops:
  0.6 20.4 %copy-start = (bf16[4,1024,256]{2,1,0:T(8,128)(2,1)S(1)}, bf16[4,1024,256]{2,1,0:T(8,128)(2,1)}, u32[]{:S(2)}) copy-start(bf16[4,1024,256]{2,1,0:T(8,128)(2,1)} %param.8) | copy-start | bytes 6291460
  17.1 7.4 %all-to-all-start.2 = ((bf16[1,4,2,4096]{3,1,0,2:T(4,128)(2,1)}), bf16[1,4,2,4096]{3,1,0,2:T(4,128)(2,1)S(1)}, u32[]{:S(2)}, u32[]{:S(2)}) async-start(bf16[1,4,2,4096]{3,1,0,2:T(4,128)(2,1)} %bitcast.30), calls=%async_computation.2 | async-start | bytes 131072 | tf_op jit(solution)/shard_map/all_to_all | solution.py:77
  24.5 30.2 %all-to-all-start.1 = ((bf16[4,1024,256]{2,1,0:T(8,128)(2,1)}), bf16[4,1024,256]{2,1,0:T(8,128)(2,1)}, u32[]{:S(2)}, u32[]{:S(2)}) async-start(bf16[4,1024,256]{2,1,0:T(8,128)(2,1)} %gather_fusion), calls=%async_computation.1 | async-start | bytes 4194304 | tf_op jit(solution)/shard_map/all_to_all | solution.py:70
  54.7 98.8 %all-to-all-start = ((bf16[4,1024,1024]{2,1,0:T(8,128)(2,1)}), bf16[4,1024,1024]{2,1,0:T(8,128)(2,1)}, u32[]{:S(2)}, u32[]{:S(2)}) async-start(bf16[4,1024,1024]{2,1,0:T(8,128)(2,1)} %pad_maximum_fusion), calls=%async_computation | async-start | bytes 16777216 | tf_op jit(solution)/shard_map/all_to_all | solution.py:69
  60.4 4.6 %copy-start.1 = (u32[32]{0:T(128)S(1)}, u32[32]{0:T(128)}, u32[]{:S(2)}) copy-start(u32[32]{0:T(128)} %constant.26) | copy-start | bytes 388
  168.4 10.5 %all-to-all-start.4 = ((bf16[4,2,128]{2,1,0:T(2,128)(2,1)}), bf16[4,2,128]{2,1,0:T(2,128)(2,1)S(1)}, u32[]{:S(2)}, u32[]{:S(2)}) async-start(bf16[4,2,128]{2,1,0:T(2,128)(2,1)} %reshape.255), calls=%async_computation.4 | async-start | bytes 4096 | tf_op jit(solution)/shard_map/all_to_all | solution.py:91
  178.8 8.8 %all-to-all-start.3 = ((bf16[4,2,512]{2,1,0:T(2,128)(2,1)}), bf16[4,2,512]{2,1,0:T(2,128)(2,1)S(1)}, u32[]{:S(2)}, u32[]{:S(2)}) async-start(bf16[4,2,512]{2,1,0:T(2,128)(2,1)} %reshape.253), calls=%async_computation.3 | async-start | bytes 16384 | tf_op jit(solution)/shard_map/all_to_all | solution.py:90
where the time goes:
time: 192 us; the launch traced here: 191 us
  waiting for transfers between devices  97.8 us (51%)
  local copies, waits for them, and re-layouts  28.1 us (15%)
  blocking collectives  23 us (12%)
  starting transfers between devices  21.6 us (11%)
  other arithmetic  11.8 us (6%)
  matrix products  7.11 us (4%)
    all_to_all x1, waiting for transfers between devices, shards(): lax.all_to_all(query_sorted, 'section', split_axis=0, concat_axis=1, tile...  85.2 us
    gather x3, local copies, waits for them, and re-layouts, shards(): query_sorted = query_train[layer_of_section]  15.8 us
    all_gather x1, blocking collectives, shards(): lax.all_gather(hidden_states[0, 0], 'tensor', axis=0, tiled=True)  15.4 us
    unnamed x2, other arithmetic  7.75 us
    unnamed x1, blocking collectives  7.55 us
    unnamed x11, local copies, waits for them, and re-layouts  5.77 us
    all_to_all x1, starting transfers between devices, shards(): lax.all_to_all(query_sorted, 'section', split_axis=0, concat_axis=1, tile...  5.67 us
    all_to_all x1, starting transfers between devices, shards(): lax.all_to_all(key_value, 'tensor', split_axis=0, concat_axis=1, tiled=True)  4.97 us
  transfers between devices with their start and end apart: 5, of which 5 were waited for; matrix products, arithmetic and copies ran while one was open for 19% of the time, Pallas kernels for 0%

commit v1 on v0

--- a/solution.py
+++ b/solution.py
@@ -66,7 +66,15 @@
     query_sorted = query_train[layer_of_section]
     keyval_sorted = keyval_train[layer_of_section]
     moved = (
-        lax.all_to_all(query_sorted, "section", split_axis=0, concat_axis=1, tiled=True),
+        jnp.concatenate(
+            lax.all_to_all(
+                jnp.stack(jnp.split(query_sorted, lax.axis_size("section"), axis=0)),
+                "section",
+                0,
+                0,
+            ),
+            axis=1,
+        ),
         lax.all_to_all(keyval_sorted, "section", split_axis=0, concat_axis=1, tiled=True),
     )
     query_cols = moved[0].shape[2]

time: 192 us -> 217 us (1.13)
  waiting for transfers between devices: 97.8 us -> 115 us
  local copies, waits for them, and re-layouts: 28.1 us -> 38.5 us
  other arithmetic: 11.8 us -> 8.02 us
    all_to_all x1, waiting for transfers between devices: 2.26 us -> 18 us  [shards(): lax.all_to_all(keyval_sorted, 'section', split_axis=0, concat_axis=1, til...]
    unnamed x11 -> x15, local copies, waits for them, and re-layouts: 5.77 us -> 13.9 us
    unnamed x2 -> x1, other arithmetic: 7.75 us -> 0.08 us
    another operation x1 -> x2, local copies, waits for them, and re-layouts: 0.66 us -> 4.53 us  [the longest x1 3.88 us: shards(): jnp.stack(jnp.split(query_sorted, lax.axis_size('section'), axis=0))]
    another operation x1 -> x2, other arithmetic: 0.08 us -> 3.9 us  [the longest x1 3.83 us: shards(): jnp.stack(jnp.split(query_sorted, lax.axis_size('section'), axis=0))]
    all_to_all x1, waiting for transfers between devices: 85.2 us -> 87.8 us  [shards(): lax.all_to_all(jnp.stack(jnp.split(query_sorted, lax.axis_size('section')...]
  transfers between devices with their start and end apart: 5 -> 5, of which waited for: 5 -> 4; matrix products, arithmetic and copies ran while one was open for 19% -> 20% of each run, Pallas kernels for 0% -> 0%
where the time goes in v1:
time: 217 us; the launch traced here: 216 us
  waiting for transfers between devices  115 us (53%)
  local copies, waits for them, and re-layouts  38.5 us (18%)
  blocking collectives  24.4 us (11%)
  starting transfers between devices  21.6 us (10%)
  other arithmetic  8.02 us (4%)
  matrix products  7.24 us (3%)
    all_to_all x1, waiting for transfers between devices, shards(): lax.all_to_all(jnp.stack(jnp.split(query_sorted, lax.axis_size('section')...  87.8 us
    all_to_all x1, waiting for transfers between devices, shards(): lax.all_to_all(keyval_sorted, 'section', split_axis=0, concat_axis=1, til...  18 us
    gather x3, local copies, waits for them, and re-layouts, shards(): query_sorted = query_train[layer_of_section]  15.8 us
    all_gather x1, blocking collectives, shards(): lax.all_gather(hidden_states[0, 0], 'tensor', axis=0, tiled=True)  15.4 us
    unnamed x15, local copies, waits for them, and re-layouts  13.9 us
    unnamed x1, blocking collectives  9 us
    all_to_all x1, starting transfers between devices, shards(): lax.all_to_all(jnp.stack(jnp.split(query_sorted, lax.axis_size('section')...  5.63 us
    dot_general x1, matrix products, shards(): jnp.einsum('gbr,rc->gbc', arrived[:, :, 0, :], w_both, preferred_element_...  5 us
  transfers between devices with their start and end apart: 5, of which 4 were waited for; matrix products, arithmetic and copies ran while one was open for 20% of the time, Pallas kernels for 0%

profile of v1, /device:TPU:0, one launch (start us, length us, event | category | flops | bytes accessed | tf_op | source)
XLA Modules:
  0.0 215.9 jit_solution(14754524049636812660)
XLA Ops:
  0.6 0.0 copy-start
  0.6 15.4 %all-gather = bf16[4,1,1,8192]{3,2,1,0:T(2,128)(2,1)S(1)} all-gather(bf16[1,1,1,8192]{3,2,1,0:T(2,128)(2,1)} %param.6), channel_id=2, replica_groups=mesh['group'=2,'section'=4,'tensor'=4] {'tensor'}, dimensions={0}, use_global_device_ids=true | all-gather | bytes 81920 | tf_op jit(solution)/shard_map/all_gather | solution.py:65
  16.1 1.0 reduce.4
  17.1 3.3 %all-to-all-start.2 = ((bf16[1,4,2,4096]{3,1,0,2:T(4,128)(2,1)}), bf16[1,4,2,4096]{3,1,0,2:T(4,128)(2,1)S(1)}, u32[]{:S(2)}, u32[]{:S(2)}) async-start(bf16[1,4,2,4096]{3,1,0,2:T(4,128)(2,1)} %bitcast.34), calls=%async_computation.2 | async-start | bytes 131072 | tf_op jit(solution)/shard_map/all_to_all | solution.py:85
  20.4 0.7 compare_select_fusion
  21.1 5.9 %fusion.23 = (bf16[4,512,1024]{2,1,0:T(8,128)(2,1)}, bf16[4,512,1024]{2,1,0:T(8,128)(2,1)}) fusion(bf16[4,1024,1024]{2,1,0:T(8,128)(2,1)} %param.7), kind=kLoop, calls=%fused_computation.59 | loop fusion | bytes 16777216 | tf_op jit(solution)/shard_map/gather | solution.py:66
  27.0 4.9 %gather_fusion.1 = bf16[4,512,1024]{2,1,0:T(8,128)(2,1)} fusion(bf16[4,512,1024]{2,1,0:T(8,128)(2,1)} %get-tuple-element.7, s32[1024]{0:T(1024)S(1)} %pad_clamp_fusion), kind=kCustom, calls=%fused_computation.1 | custom fusion | bytes 8388624 | tf_op jit(solution)/shard_map/gather | solution.py:66
  31.9 4.6 %constant_dynamic-update-slice_fusion.1 = bf16[4,1024,1024]{2,1,0:T(8,128)(2,1)} fusion(bf16[4,512,1024]{2,1,0:T(8,128)(2,1)} %gather_fusion.1), kind=kLoop, calls=%fused_computation.33 | loop fusion | bytes 8388608
  36.5 4.9 %gather_fusion.2 = bf16[4,512,1024]{2,1,0:T(8,128)(2,1)} fusion(bf16[4,512,1024]{2,1,0:T(8,128)(2,1)} %get-tuple-element.6, s32[1024]{0:T(1024)S(1)} %pad_clamp_fusion), kind=kCustom, calls=%fused_computation.2 | custom fusion | bytes 8388624 | tf_op jit(solution)/shard_map/gather | solution.py:66
  41.5 4.6 %constant_dynamic-update-slice_fusion = bf16[4,1024,1024]{2,1,0:T(8,128)(2,1)} fusion(bf16[4,1024,1024]{2,1,0:T(8,128)(2,1)} %constant_dynamic-update-slice_fusion.1, bf16[4,512,1024]{2,1,0:T(8,128)(2,1)} %gather_fusion.2), kind=kLoop, calls=%fused_computation.32 | loop fusion | bytes 8388608
  46.1 0.0 copy-done
  46.1 2.0 gather_fusion
  48.0 0.0 all-to-all-done.2
  48.0 4.4 %all-to-all-start.1 = ((bf16[4,1024,256]{2,1,0:T(8,128)(2,1)}), bf16[4,1024,256]{2,1,0:T(8,128)(2,1)}, u32[]{:S(2)}, u32[]{:S(2)}) async-start(bf16[4,1024,256]{2,1,0:T(8,128)(2,1)} %gather_fusion), calls=%async_computation.1 | async-start | bytes 4194304 | tf_op jit(solution)/shard_map/all_to_all | solution.py:78
  52.5 3.9 %slice_bitcast_fusion.3 = (bf16[1,1,1024,1024]{3,2,1,0:T(8,128)(2,1)S(1)}, bf16[1,1,1024,1024]{3,2,1,0:T(8,128)(2,1)S(1)}, bf16[1,1,1024,1024]{3,2,1,0:T(8,128)(2,1)S(1)}, bf16[1,1,1024,1024]{3,2,1,0:T(8,128)(2,1)S(1)}) fusion(bf16[4,1024,1024]{2,1,0:T(8,128)(2,1)} %constant_dynamic-update-slice_fusion), kind=kLoop, calls=%fused_computation.10 | loop fusion | bytes 16777216 | tf_op jit(solution)/shard_map/stack | solution.py:71
  56.4 3.8 %pad_maximum_fusion = bf16[4,1,1024,1024]{3,2,1,0:T(8,128)(2,1)} fusion(bf16[1,1,1024,1024]{3,2,1,0:T(8,128)(2,1)S(1)} %get-tuple-element.3, bf16[1,1,1024,1024]{3,2,1,0:T(8,128)(2,1)S(1)} %get-tuple-element.4, bf16[1,1,1024,1024]{3,2,1,0:T(8,128)(2,1)S(1)} %get-tuple-element.5, bf16[1,1,1024,1024]{3,2,1,0:T(8,128)(2,1)S(1)} %get-tuple-element.2), kind=kLoop, calls=%fused_computation.5 | loop fusion | flops 12582912 | bytes 16777216 | tf_op jit(solution)/shard_map/stack | solution.py:71
  60.2 18.0 %all-to-all-done.1 = bf16[4,1024,256]{2,1,0:T(8,128)(2,1)} async-done(((bf16[4,1024,256]{2,1,0:T(8,128)(2,1)}), bf16[4,1024,256]{2,1,0:T(8,128)(2,1)}, u32[]{:S(2)}, u32[]{:S(2)}) %all-to-all-start.1) | async-done | bytes 2097184 | tf_op jit(solution)/shard_map/all_to_all | solution.py:78
  78.2 5.6 %all-to-all-start = ((bf16[4,1,1024,1024]{3,2,1,0:T(8,128)(2,1)}), bf16[4,1,1024,1024]{3,2,1,0:T(8,128)(2,1)}, u32[]{:S(2)}, u32[]{:S(2)}) async-start(bf16[4,1,1024,1024]{3,2,1,0:T(8,128)(2,1)} %pad_maximum_fusion), calls=%async_computation | async-start | bytes 16777216 | tf_op jit(solution)/shard_map/all_to_all | solution.py:70
  83.9 0.0 copy-start.2
  84.5 2.9 %copy.14 = bf16[1,1,1,1024,1024]{3,4,2,1,0:T(8,128)(2,1)S(1)} copy(bf16[1,1,1,1024,1024]{4,3,2,1,0:T(8,128)(2,1)} %param.11) | data formatting | bytes 4194304 | tf_op args[5]
  87.4 0.0 copy-done.2
  87.4 0.6 dynamic-slice
  88.1 1.2 fusion.24
  89.2 87.8 %all-to-all-done = bf16[4,1,1024,1024]{3,2,1,0:T(8,128)(2,1)} async-done(((bf16[4,1,1024,1024]{3,2,1,0:T(8,128)(2,1)}), bf16[4,1,1024,1024]{3,2,1,0:T(8,128)(2,1)}, u32[]{:S(2)}, u32[]{:S(2)}) %all-to-all-start) | async-done | bytes 8388640 | tf_op jit(solution)/shard_map/all_to_all | solution.py:70
  177.0 0.0 copy-start.1
  177.0 5.0 %fusion.1 = f32[2,4,1280]{2,1,0:T(4,128)S(1)} fusion(bf16[4096,256]{1,0:T(8,128)(2,1)} %bitcast.6, bf16[4096,1024]{1,0:T(8,128)(2,1)} %bitcast.5, bf16[1,4,2,4096]{3,1,0,2:T(4,128)(2,1)S(1)} %all-to-all-done.2), kind=kOutput, calls=%fused_computation.6 | convolution fusion | flops 104857600 | bytes 10592256 | tf_op jit(solution)/shard_map/gbr,rc->gbc/dot_general | solution.py:88
  182.0 9.0 %all-reduce = bf16[2,4,1280]{2,1,0:T(4,128)(2,1)S(1)} all-reduce(f32[2,4,1280]{2,1,0:T(4,128)S(1)} %fusion.1), channel_id=3, replica_groups=mesh['group'=2,'section'=4,'tensor'=4] {'group'}, use_global_device_ids=true, to_apply=%region_0.0.clone | all-reduce | flops 10240 | bytes 61440
  191.0 0.7 fusion.10
  191.7 0.5 broadcast.87
  192.2 0.7 reduce.6
  192.9 0.6 reshape.251
  193.5 5.0 %all-to-all-start.4 = ((bf16[4,2,128]{2,1,0:T(2,128)(2,1)}), bf16[4,2,128]{2,1,0:T(2,128)(2,1)S(1)}, u32[]{:S(2)}, u32[]{:S(2)}) async-start(bf16[4,2,128]{2,1,0:T(2,128)(2,1)} %reshape.251), calls=%async_computation.4 | async-start | bytes 4096 | tf_op jit(solution)/shard_map/all_to_all | solution.py:99
  198.4 0.7 reduce.5
  199.1 0.6 reshape.249
  199.7 4.2 %all-to-all-done.4 = bf16[4,2,128]{2,1,0:T(2,128)(2,1)S(1)} async-done(((bf16[4,2,128]{2,1,0:T(2,128)(2,1)}), bf16[4,2,128]{2,1,0:T(2,128)(2,1)S(1)}, u32[]{:S(2)}, u32[]{:S(2)}) %all-to-all-start.4) | async-done | bytes 2080 | tf_op jit(solution)/shard_map/all_to_all | solution.py:99
  203.9 3.2 %all-to-all-start.3 = ((bf16[4,2,512]{2,1,0:T(2,128)(2,1)}), bf16[4,2,512]{2,1,0:T(2,128)(2,1)S(1)}, u32[]{:S(2)}, u32[]{:S(2)}) async-start(bf16[4,2,512]{2,1,0:T(2,128)(2,1)} %reshape.249), calls=%async_computation.3 | async-start | bytes 16384 | tf_op jit(solution)/shard_map/all_to_all | solution.py:98
  207.2 0.1 subtract_convert_fusion.1
  207.3 0.1 maximum_bitcast_fusion.6
  207.4 0.6 maximum_bitcast_fusion.4
  208.0 0.1 maximum_bitcast_fusion.5
  208.0 4.7 %all-to-all-done.3 = bf16[4,2,512]{2,1,0:T(2,128)(2,1)S(1)} async-done(((bf16[4,2,512]{2,1,0:T(2,128)(2,1)}), bf16[4,2,512]{2,1,0:T(2,128)(2,1)S(1)}, u32[]{:S(2)}, u32[]{:S(2)}) %all-to-all-start.3) | async-done | bytes 8224 | tf_op jit(solution)/shard_map/all_to_all | solution.py:98
  212.8 0.1 fusion.11
  212.9 0.2 fusion.13
  213.0 1.6 fusion.26
  214.7 0.2 fusion.4
  214.9 0.4 fusion.3
  215.3 0.6 convert_element_type.77
  215.9 0.0 copy-done.1
  (12 shorter events, 0.2 us)
Async XLA Ops:
  0.6 45.4 %copy-start = (bf16[4,1024,256]{2,1,0:T(8,128)(2,1)S(1)}, bf16[4,1024,256]{2,1,0:T(8,128)(2,1)}, u32[]{:S(2)}) copy-start(bf16[4,1024,256]{2,1,0:T(8,128)(2,1)} %param.8) | copy-start | bytes 6291460
  17.1 30.9 %all-to-all-start.2 = ((bf16[1,4,2,4096]{3,1,0,2:T(4,128)(2,1)}), bf16[1,4,2,4096]{3,1,0,2:T(4,128)(2,1)S(1)}, u32[]{:S(2)}, u32[]{:S(2)}) async-start(bf16[1,4,2,4096]{3,1,0,2:T(4,128)(2,1)} %bitcast.34), calls=%async_computation.2 | async-start | bytes 131072 | tf_op jit(solution)/shard_map/all_to_all | solution.py:85
  48.0 30.2 %all-to-all-start.1 = ((bf16[4,1024,256]{2,1,0:T(8,128)(2,1)}), bf16[4,1024,256]{2,1,0:T(8,128)(2,1)}, u32[]{:S(2)}, u32[]{:S(2)}) async-start(bf16[4,1024,256]{2,1,0:T(8,128)(2,1)} %gather_fusion), calls=%async_computation.1 | async-start | bytes 4194304 | tf_op jit(solution)/shard_map/all_to_all | solution.py:78
  78.2 98.8 %all-to-all-start = ((bf16[4,1,1024,1024]{3,2,1,0:T(8,128)(2,1)}), bf16[4,1,1024,1024]{3,2,1,0:T(8,128)(2,1)}, u32[]{:S(2)}, u32[]{:S(2)}) async-start(bf16[4,1,1024,1024]{3,2,1,0:T(8,128)(2,1)} %pad_maximum_fusion), calls=%async_computation | async-start | bytes 16777216 | tf_op jit(solution)/shard_map/all_to_all | solution.py:70
  83.9 3.6 %copy-start.2 = (u32[32]{0:T(128)S(1)}, u32[32]{0:T(128)}, u32[]{:S(2)}) copy-start(u32[32]{0:T(128)} %constant.26) | copy-start | bytes 388
  177.0 38.9 %copy-start.1 = (bf16[4,1024,256]{2,1,0:T(8,128)(2,1)S(1)}, bf16[4,1024,256]{2,1,0:T(8,128)(2,1)}, u32[]{:S(2)}) copy-start(bf16[4,1024,256]{2,1,0:T(8,128)(2,1)} %param.8) | copy-start | bytes 6291460
  193.5 10.5 %all-to-all-start.4 = ((bf16[4,2,128]{2,1,0:T(2,128)(2,1)}), bf16[4,2,128]{2,1,0:T(2,128)(2,1)S(1)}, u32[]{:S(2)}, u32[]{:S(2)}) async-start(bf16[4,2,128]{2,1,0:T(2,128)(2,1)} %reshape.251), calls=%async_computation.4 | async-start | bytes 4096 | tf_op jit(solution)/shard_map/all_to_all | solution.py:99
  203.9 8.8 %all-to-all-start.3 = ((bf16[4,2,512]{2,1,0:T(2,128)(2,1)}), bf16[4,2,512]{2,1,0:T(2,128)(2,1)S(1)}, u32[]{:S(2)}, u32[]{:S(2)}) async-start(bf16[4,2,512]{2,1,0:T(2,128)(2,1)} %reshape.249), calls=%async_computation.3 | async-start | bytes 16384 | tf_op jit(solution)/shard_map/all_to_all | solution.py:98
